TPU v7x, 32 devices: a whole 2x2x4 slice. The times are simulated.
32 devices in a mesh: groups: 2 (over y), seq: 4 (over z), heads: 2 (over x), cfg: 2 (over core).
Axes of the slice: x: 2, y: 2, z: 4, core: 2. Of those that a mesh axis runs over, the one named last changes fastest.
Arguments:
- video_tokens: bfloat16 [2, 8, 1152, 1024], P('cfg', ('groups', 'seq'), 'heads'), parts along dimension 1, may hold values from -6 to 6
- text_tokens: bfloat16 [2, 8, 1152, 128], P('cfg', ('groups', 'seq'), 'heads'), parts along dimension 1, may hold values from -6 to 6
- text_length: int32 [2, 8], P('cfg', ('groups', 'seq')), parts along dimension 1, may hold values from 1 to 128
- guide_numer: int32 [8], P(('groups', 'seq')), parts along dimension 0, may hold values from 2 to 8
- guide_denom: int32 [8], P(('groups', 'seq')), parts along dimension 0, may hold values from 4 to 8
- spatial_gain: bfloat16 [1152], replicated, may hold values from 0.25 to 1.75
- spatial_qkv: bfloat16 [3, 1152, 1152], P(None, 'heads'), may hold values from -0.11785113 to 0.11785113
- spatial_out: bfloat16 [1152, 1152], P('heads'), may hold values from -0.1875 to 0.1875
- temporal_gain: bfloat16 [1152], replicated, may hold values from 0.25 to 1.75
- temporal_qkv: bfloat16 [3, 1152, 1152], P(None, 'heads'), may hold values from -0.11785113 to 0.11785113
- temporal_out: bfloat16 [1152, 1152], P('heads'), may hold values from -0.1875 to 0.1875
Outputs:
- guided: bfloat16 [8, 1152, 1024], P(('groups', 'seq'), ('heads', 'cfg')), parts along dimension 0
There are 2 independent parts, one for each index of `groups`. A program takes and returns all parts, laid end to end along the dimension named above; an argument that names none is the same for every part. Nothing has to cross between parts.
Inputs may be any that keep to these rules, and one draw needn't show every extreme that they name: `text_length`: text tokens at or beyond a frame's length are padding.
All inputs are finite; a program needn't handle non-finite values.
Results may differ from a plain program's by a relative error of at most 0.009.
Values may be sent and summed in bfloat16 or wider, within the bound.
A program may use at most 64 MiB of HBM per device.

v0:
```python
import jax
import jax.numpy as jnp
from jax import lax
from jax.sharding import PartitionSpec as P

D = 1152
HEAD_DIM = 72
epsilon = 1e-06


def from_partner(shard, axis, stride):
    return lax.ppermute(shard, axis, [(i, i ^ 1 << stride) for i in range(lax.axis_size(axis))])


def softmax_along(scores, axis):
    top_score = jnp.max(scores, axis=axis, keepdims=True)
    expons = jnp.exp(scores - top_score)
    return (expons / jnp.sum(expons, axis=axis, keepdims=True)).astype(jnp.bfloat16)


def project_piece(piece, gain_vector, weights, parts):
    gain_piece = gain_vector.astype(jnp.float32)
    weight_piece = weights[parts]
    piece_wide = piece.astype(jnp.float32)
    scaled = (piece_wide * gain_piece[None, :, None]).astype(jnp.bfloat16)
    product = jnp.einsum("kod,fdp->fkop", weight_piece, scaled, preferred_element_type=jnp.float32)
    return (product, jnp.sum(piece_wide * piece_wide, axis=1))


def add_mixed(piece, matrix):
    return jnp.einsum("oc,fcp->fop", matrix, piece, preferred_element_type=jnp.float32)


def shards(
    video_tokens,
    text_tokens,
    text_length,
    guide_numer,
    guide_denom,
    spatial_gain,
    spatial_qkv,
    spatial_out,
    temporal_gain,
    temporal_qkv,
    temporal_out,
):
    frame_count = video_tokens.shape[1]
    width = video_tokens.shape[2]
    positions = video_tokens.shape[3]
    text_count = text_tokens.shape[3]
    local_heads = width // HEAD_DIM
    frame_tokens = video_tokens[0]
    frame_text = text_tokens[0]
    video_piece = lax.all_gather(frame_tokens, "heads", axis=1, tiled=True)
    text_piece = lax.all_gather(frame_text, "heads", axis=1, tiled=True)
    video_add, video_sq = project_piece(video_piece, spatial_gain, spatial_qkv, slice(0, 3))
    text_add, text_sq = project_piece(text_piece, spatial_gain, spatial_qkv, slice(1, 3))
    mixed = (video_add * lax.rsqrt(video_sq / D + epsilon)[:, None, None, :]).astype(jnp.bfloat16)
    mixed = mixed.reshape(frame_count, 3, local_heads, HEAD_DIM, positions)
    context = (text_add * lax.rsqrt(text_sq / D + epsilon)[:, None, None, :]).astype(jnp.bfloat16)
    context = context.reshape(frame_count, 2, local_heads, HEAD_DIM, text_count)
    key_rows = jnp.concatenate([mixed[:, 1], context[:, 0]], axis=3)
    value_rows = jnp.concatenate([mixed[:, 2], context[:, 1]], axis=3)
    query_all = mixed[:, 0]
    text_valid = jnp.arange(text_count, dtype=jnp.int32)[None, :] < text_length[0][:, None]
    valid_keys = jnp.concatenate(
        [jnp.ones((frame_count, positions), dtype=bool), text_valid], axis=1
    )
    block_rows = min(512, positions)
    block_count = positions // block_rows
    frame_ids = jnp.repeat(jnp.arange(frame_count, dtype=jnp.int32), block_count)
    block_ids = jnp.tile(jnp.arange(block_count, dtype=jnp.int32), frame_count)

    def block_step(inputs):
        frame_id, block_id = inputs
        query_rows = lax.dynamic_slice_in_dim(
            query_all[frame_id], block_id * block_rows, block_rows, 2
        )
        scores = jnp.einsum(
            "hep,hek->hpk", query_rows, key_rows[frame_id], preferred_element_type=jnp.float32
        )
        scores = scores * HEAD_DIM ** (-0.5)
        scores = jnp.where(valid_keys[frame_id][None, None, :], scores, -jnp.inf)
        weights = softmax_along(scores, 2)
        result = jnp.einsum(
            "hpk,hek->hep", weights, value_rows[frame_id], preferred_element_type=jnp.float32
        )
        return result.astype(jnp.bfloat16)

    attended = lax.map(block_step, (frame_ids, block_ids))
    attended = attended.reshape(frame_count, block_count, local_heads, HEAD_DIM, block_rows)
    attended = jnp.transpose(attended, (0, 2, 3, 1, 4)).reshape(frame_count, width, positions)
    update = add_mixed(lax.all_gather(attended, "heads", axis=1, tiled=True), spatial_out)
    after_spatial = (frame_tokens.astype(jnp.float32) + update).astype(jnp.bfloat16)
    own_rows = lax.all_to_all(after_spatial, "seq", split_axis=2, concat_axis=0, tiled=True)
    frames_all = own_rows.shape[0]
    columns = own_rows.shape[2]
    piece_add, piece_sq = project_piece(
        lax.all_gather(own_rows, "heads", axis=1, tiled=True),
        temporal_gain,
        temporal_qkv,
        slice(0, 3),
    )
    mixed_time = (piece_add * lax.rsqrt(piece_sq / D + epsilon)[:, None, None, :]).astype(
        jnp.bfloat16
    )
    mixed_time = mixed_time.reshape(frames_all, 3, local_heads, HEAD_DIM, columns)
    time_scores = jnp.einsum(
        "fhep,ghep->hfgp", mixed_time[:, 0], mixed_time[:, 1], preferred_element_type=jnp.float32
    )
    time_weights = softmax_along(time_scores * HEAD_DIM ** (-0.5), 2)
    attended_time = jnp.einsum(
        "hfgp,ghep->fhep", time_weights, mixed_time[:, 2], preferred_element_type=jnp.float32
    )
    attended_time = attended_time.astype(jnp.bfloat16).reshape(frames_all, width, columns)
    update_time = add_mixed(
        lax.all_gather(attended_time, "heads", axis=1, tiled=True), temporal_out
    )
    block_out = (own_rows.astype(jnp.float32) + update_time).astype(jnp.bfloat16)
    returned = lax.all_to_all(block_out, "seq", split_axis=0, concat_axis=2, tiled=True)
    half_width = width // 2
    partner = from_partner(returned, "cfg", 0)
    branch_index = lax.axis_index("cfg")
    cond_full = jnp.where(branch_index == 0, returned, partner)
    uncond_full = jnp.where(branch_index == 0, partner, returned)
    cond_part = lax.dynamic_slice_in_dim(cond_full, branch_index * half_width, half_width, 1)
    uncond_part = lax.dynamic_slice_in_dim(uncond_full, branch_index * half_width, half_width, 1)
    ratio = guide_numer.astype(jnp.float32) / guide_denom.astype(jnp.float32)
    cond_wide = cond_part.astype(jnp.float32)
    uncond_wide = uncond_part.astype(jnp.float32)
    return (uncond_wide + ratio[:, None, None] * (cond_wide - uncond_wide)).astype(jnp.bfloat16)


def solution(mesh):
    return jax.shard_map(
        shards,
        mesh=mesh,
        in_specs=(
            P("cfg", ("groups", "seq"), "heads", None),
            P("cfg", ("groups", "seq"), "heads", None),
            P("cfg", ("groups", "seq")),
            P(("groups", "seq")),
            P(("groups", "seq")),
            P(),
            P(None, "heads", None),
            P("heads", None),
            P(),
            P(None, "heads", None),
            P("heads", None),
        ),
        out_specs=P(("groups", "seq"), ("heads", "cfg"), None),
        check_vma=False,
    )
```

profile of v0, /device:TPU:0, one launch (start us, length us, event | category | flops | bytes accessed | tf_op | source)
XLA Modules:
  0.0 359.0 jit_solution(843548291912899709)
XLA Ops:
  6.5 0.0 copy-start
  6.5 0.0 all-gather.12.cloned.1.call-start
  6.5 0.7 all-gather.12.cloned.1.call-update
  7.3 0.0 all-gather.8.cloned.1.call-start
  7.3 0.7 convert_element_type.98
  8.7 7.7 %all-gather.1 = bf16[1,1,1152,128]{3,2,1,0:T(8,128)(2,1)S(1)} all-gather(bf16[1,1,576,128]{3,2,1,0:T(8,128)(2,1)} %param.14), channel_id=3, replica_groups=mesh['groups'=2,'seq'=4,'heads'=2,'cfg'=2] {'heads'}, dimensions={2}, use_global_device_ids=true | all-gather | bytes 442368 | tf_op jit(solution)/shard_map/all_gather | solution.py:55
  16.4 0.2 fusion.93
  16.6 3.0 fusion.87
  19.6 28.1 %all-gather.12.cloned.1.call-done = bf16[1,1,1152,1024]{3,2,1,0:T(8,128)(2,1)} async-done(((bf16[1,1,576,1024]{3,2,1,0:T(8,128)(2,1)}), bf16[1,1,1152,1024]{3,2,1,0:T(8,128)(2,1)}) %all-gather.12.cloned.1.call-update) | async-done | bytes 2359312 | tf_op jit(solution)/shard_map/all_gather | solution.py:54
  47.7 2.3 fusion.50
  50.0 0.0 copy-done.3
  50.1 7.3 %fusion.48 = bf16[1,1024,3,576]{1,3,2,0:T(8,128)(2,1)S(1)} fusion(f32[1024]{0:T(1024)S(1)} %add_rsqrt_fusion.1, bf16[3,576,1152]{2,1,0:T(8,128)(2,1)} %param.19, bf16[1,1,1152,1024]{3,2,1,0:T(8,128)(2,1)S(1)} %copy-done.3, f32[1152]{0:T(1024)S(1)} %convert_element_type.98), kind=kOutput, calls=%fused_computation.28 | convolution fusion | flops 4083941376 | bytes 9888256 | tf_op jit(solution)/shard_map/kod,fdp->fkop/dot_general | solution.py:26
  57.3 1.4 slice_bitcast_fusion
  58.7 1.3 pad_maximum_fusion
  60.1 37.0 %while.10 = (s32[]{:T(128)}, bf16[2,8,72,512]{3,2,1,0:T(8,128)(2,1)}, pred[1,1152]{1,0:T(4,128)(4,1)S(1)}, s32[2]{0:T(128)S(1)}, bf16[1,8,72,1024]{3,2,1,0:T(8,1...) while((s32[]{:T(128)}, ...), condition=%wide.region_5.6_spmd, body=%wide.region_2.5_spmd.sunk | while | flops 2081200384 | bytes 5788856 | solution.py:90
  60.5 0.7 dynamic_slice.50
  61.9 7.0 %exponential_reduce_fusion.2 = f32[8,512]{1,0:T(8,128)S(1)} fusion(pred[1152]{0:T(1024)(128)(4,1)S(1)} %reduce.5, bf16[1,8,72,1152]{3,2,1,0:T(8,128)(2,1)S(1)} %get-tuple-element.139, bf16[1,8,72,1024]{3,2,1,0:T(8,128)(2,1)} %get-tuple-element.138, s32[]{:T(128)S(6)} %select_n.52), kind=kOutput, calls=%fused_computation.5.clone.1 | convolution fusion | flops 698352768 | bytes 1934468 | tf_op jit(solution)/shard_map/while/body/eval_jaxpr/sub | solution.py:17
  69.0 9.8 %fusion.120 = bf16[2,8,72,512]{3,2,1,0:T(8,128)(2,1)} fusion(bf16[2,8,72,512]{3,2,1,0:T(8,128)(2,1)} %get-tuple-element.123, s32[]{:T(128)} %get-tuple-element.122, bf16[1,8,72,1152]{3,2,1,0:T(8,128)(2,1)} %get-tuple-element.140, f32[8,512]{1,0:T(8,128)S(1)} %exponential_reduce_fusion.2, pred[1152]{0:T(1024)(128)(4,1)S(1)} %reduce.5, ...), kind=kOutput, calls=%fused_computation.13.clone.1 | convolution fusion | flops 1382847616 | bytes 3851908 | tf_op jit(solution)/shard_map/while/body/eval_jaxpr/hpk,hek->hep/dot_general | solution.py:85
  78.8 0.7 dynamic_slice.50
  80.2 7.0 %exponential_reduce_fusion.2 = f32[8,512]{1,0:T(8,128)S(1)} fusion(pred[1152]{0:T(1024)(128)(4,1)S(1)} %reduce.5, bf16[1,8,72,1152]{3,2,1,0:T(8,128)(2,1)S(1)} %get-tuple-element.139, bf16[1,8,72,1024]{3,2,1,0:T(8,128)(2,1)} %get-tuple-element.138, s32[]{:T(128)S(6)} %select_n.52), kind=kOutput, calls=%fused_computation.5.clone.1 | convolution fusion | flops 698352768 | bytes 1934468 | tf_op jit(solution)/shard_map/while/body/eval_jaxpr/sub | solution.py:17
  87.2 9.8 %fusion.120 = bf16[2,8,72,512]{3,2,1,0:T(8,128)(2,1)} fusion(bf16[2,8,72,512]{3,2,1,0:T(8,128)(2,1)} %get-tuple-element.123, s32[]{:T(128)} %get-tuple-element.122, bf16[1,8,72,1152]{3,2,1,0:T(8,128)(2,1)} %get-tuple-element.140, f32[8,512]{1,0:T(8,128)S(1)} %exponential_reduce_fusion.2, pred[1152]{0:T(1024)(128)(4,1)S(1)} %reduce.5, ...), kind=kOutput, calls=%fused_computation.13.clone.1 | convolution fusion | flops 1382847616 | bytes 3851908 | tf_op jit(solution)/shard_map/while/body/eval_jaxpr/hpk,hek->hep/dot_general | solution.py:85
  97.1 2.5 copy.43
  99.6 1.7 reshape.105
  101.2 0.0 all-gather.8.cloned.1.call-update
  101.3 0.2 all-gather.14.cloned.1.call-start
  101.5 36.0 %all-gather.8.cloned.1.call-done = bf16[1,1152,1024]{2,1,0:T(8,128)(2,1)} async-done(((bf16[1,576,1024]{2,1,0:T(8,128)(2,1)}), bf16[1,1152,1024]{2,1,0:T(8,128)(2,1)}) %all-gather.8.cloned.1.call-update) | async-done | bytes 2359312 | tf_op jit(solution)/shard_map/all_gather | solution.py:93
  137.5 0.0 copy-done
  137.5 3.7 %fusion.64 = bf16[1,576,1024]{2,1,0:T(8,128)(2,1)S(1)} fusion(bf16[576,1152]{1,0:T(8,128)(2,1)S(1)} %copy-done, bf16[1,1152,1024]{2,1,0:T(8,128)(2,1)} %all-gather.8.cloned.1.call-done, bf16[1,1,576,1024]{3,2,1,0:T(8,128)(2,1)} %param.13), kind=kOutput, calls=%fused_computation.47 | convolution fusion | flops 1360723968 | bytes 6045696 | tf_op jit(solution)/shard_map/oc,fcp->fop/dot_general | solution.py:31
  141.1 4.1 %copy.44 = bf16[1,576,1024]{1,0,2:T(2,128)(2,1)} copy(bf16[1,576,1024]{2,1,0:T(8,128)(2,1)S(1)} %fusion.64) | data formatting | bytes 2359296 | tf_op jit(solution)/shard_map/convert_element_type | solution.py:94
  145.3 0.5 broadcast.82
  145.8 9.9 %reduce.3 = bf16[1024,576]{1,0:T(8,128)(2,1)S(1)} reduce(bf16[1024,1,576]{2,1,0:T(2,128)(2,1)} %bitcast.189, bf16[]{:T(256)} %broadcast.82), dimensions={1}, to_apply=%bitcast.164.reduce_sub_computation | reduce | bytes 2359298
  155.7 2.6 reshape.124
  158.3 33.0 %all_to_all.36 = bf16[4,2,73728]{2,1,0:T(2,128)(2,1)S(1)} all-to-all(bf16[4,2,73728]{2,1,0:T(2,128)(2,1)} %reshape.124), channel_id=1, replica_groups=mesh['groups'=2,'seq'=4,'heads'=2,'cfg'=2] {'seq'}, dimensions={0} | all-to-all | bytes 2359296 | tf_op jit(solution)/shard_map/all_to_all | solution.py:95
  191.3 3.3 reshape.125
  194.5 1.9 copy.57
  196.5 0.0 copy-start.5
  196.5 1.5 copy.46
  197.9 0.0 all-gather.14.cloned.1.call-update
  198.0 0.3 all-gather.10.cloned.1.call-start
  198.2 0.0 copy-done.5
  198.3 34.1 %all-gather.14.cloned.1.call-done = bf16[4,1,1152,256]{3,2,0,1:T(8,128)(2,1)} async-done(((bf16[4,1,576,256]{3,2,0,1:T(8,128)(2,1)}), bf16[4,1,1152,256]{3,2,0,1:T(8,128)(2,1)}) %all-gather.14.cloned.1.call-update) | async-done | bytes 2359312 | tf_op jit(solution)/shard_map/all_gather | solution.py:99
  232.3 2.3 fusion.52
  234.6 0.1 copy-done.4
  234.7 7.2 %multiply_convert_fusion = bf16[4,256,3,576]{1,3,2,0:T(8,128)(2,1)S(1)} fusion(f32[4,256]{1,0:T(4,128)S(1)} %add_rsqrt_fusion, bf16[3,576,1152]{2,1,0:T(8,128)(2,1)} %param.22, bf16[4,1,1152,256]{3,2,0,1:T(8,128)(2,1)S(1)} %copy-done.4, f32[1152]{0:T(1024)S(1)} %convert_element_type.109), kind=kOutput, calls=%fused_computation.29 | convolution fusion | flops 4083941376 | bytes 9888256 | tf_op jit(solution)/shard_map/kod,fdp->fkop/dot_general | solution.py:26
  241.9 1.9 fusion.104
  243.8 2.8 copy.59
  246.7 4.1 %copy.60 = bf16[4,1,8,72,256]{3,0,4,2,1:T(4,128)(2,1)} copy(bf16[4,1,8,72,256]{4,3,2,1,0:T(8,128)(2,1)} %get-tuple-element.59) | data formatting | bytes 2359296
  250.7 5.8 %fusion.71 = f32[8,256,4,4]{3,2,1,0:T(4,128)} fusion(bf16[4,1,8,72,256]{3,0,4,2,1:T(4,128)(2,1)} %copy.60, bf16[4,1,8,72,256]{3,0,4,2,1:T(4,128)(2,1)S(1)} %copy.59), kind=kOutput, calls=%fused_computation.54 | convolution fusion | flops 4718592 | bytes 2490368 | tf_op jit(solution)/shard_map/fhep,ghep->hfgp/dot_general | solution.py:108
  256.5 2.8 copy.50
  259.4 0.0 copy-start.1
  259.5 2.1 copy.51
  261.6 0.0 copy-done.1
  261.6 2.5 copy.58
  264.1 5.8 %convert_bitcast_fusion = bf16[4,8,72,256]{2,0,3,1:T(4,128)(2,1)} fusion(bf16[8,4,4,256]{2,1,3,0:T(4,128)(2,1)} %copy.51, bf16[4,1,8,72,256]{3,0,4,2,1:T(4,128)(2,1)} %copy.58), kind=kOutput, calls=%fused_computation.59 | convolution fusion | flops 5308416 | bytes 2424832 | tf_op jit(solution)/shard_map/hfgp,ghep->fhep/dot_general | solution.py:112
  269.9 4.2 %copy.52 = bf16[4,8,72,256]{3,2,1,0:T(8,128)(2,1)} copy(bf16[4,8,72,256]{2,0,3,1:T(4,128)(2,1)} %convert_bitcast_fusion) | data formatting | bytes 2359296 | tf_op jit(solution)/shard_map/convert_element_type | solution.py:115
  274.1 0.0 all-gather.10.cloned.1.call-update
  274.1 36.2 %all-gather.10.cloned.1.call-done = bf16[4,1152,256]{2,1,0:T(8,128)(2,1)} async-done(((bf16[4,576,256]{2,1,0:T(8,128)(2,1)}), bf16[4,1152,256]{2,1,0:T(8,128)(2,1)}) %all-gather.10.cloned.1.call-update) | async-done | bytes 2359312 | tf_op jit(solution)/shard_map/all_gather | solution.py:117
  310.3 0.0 copy-done.2
  310.3 3.8 %fusion.63 = bf16[4,576,256]{2,1,0:T(8,128)(2,1)S(1)} fusion(bf16[4,1152,256]{2,1,0:T(8,128)(2,1)} %all-gather.10.cloned.1.call-done, bf16[576,1152]{1,0:T(8,128)(2,1)} %param.23, bf16[1,576,4,256]{3,1,2,0:T(8,128)(2,1)S(1)} %copy-done.2), kind=kOutput, calls=%fused_computation.45 | convolution fusion | flops 1360723968 | bytes 6045696 | tf_op jit(solution)/shard_map/oc,fcp->fop/dot_general | solution.py:31
  314.1 32.8 %all_to_all.37 = bf16[4,576,256]{2,1,0:T(8,128)(2,1)S(1)} all-to-all(bf16[4,576,256]{2,1,0:T(8,128)(2,1)S(1)} %fusion.63), channel_id=1, replica_groups=mesh['groups'=2,'seq'=4,'heads'=2,'cfg'=2] {'seq'}, dimensions={0} | all-to-all | bytes 2359296 | tf_op jit(solution)/shard_map/all_to_all | solution.py:120
  346.8 0.1 copy.61
  347.0 0.1 collective-permute-start
  348.4 1.6 collective-permute-done
  350.0 2.2 fusion.91
  (17 shorter events, 0.2 us)
Async XLA Ops:
  6.5 130.9 %copy-start = (bf16[576,1152]{1,0:T(8,128)(2,1)S(1)}, bf16[576,1152]{1,0:T(8,128)(2,1)}, u32[]{:S(2)}) copy-start(bf16[576,1152]{1,0:T(8,128)(2,1)} %param.20) | copy-start | bytes 3981316
  6.5 41.1 %all-gather.12.cloned.1.call-start = ((), (), s32[]{:S(2)}) async-start(), calls=%async_computation.4 | async-start | bytes 3538944 | tf_op jit(solution)/shard_map/all_gather | solution.py:54
  7.3 130.2 %all-gather.8.cloned.1.call-start = ((), (), s32[]{:S(2)}) async-start(), calls=%async_computation.2 | async-start | bytes 3538944 | tf_op jit(solution)/shard_map/all_gather | solution.py:93
  47.7 2.4 copy-start.3
  101.3 131.0 %all-gather.14.cloned.1.call-start = ((), (), s32[]{:S(2)}) async-start(), calls=%async_computation.5 | async-start | bytes 3538944 | tf_op jit(solution)/shard_map/all_gather | solution.py:99
  196.5 1.8 copy-start.5
  198.0 112.3 %all-gather.10.cloned.1.call-start = ((), (), s32[]{:S(2)}) async-start(), calls=%async_computation.3 | async-start | bytes 3538944 | tf_op jit(solution)/shard_map/all_gather | solution.py:117
  232.3 2.4 copy-start.4
  259.4 2.2 copy-start.1
  269.9 40.4 %copy-start.2 = (bf16[1,576,4,256]{3,1,2,0:T(8,128)(2,1)S(1)}, bf16[1,576,4,256]{3,1,2,0:T(8,128)(2,1)}, u32[]{:S(2)}) copy-start(bf16[1,576,4,256]{3,1,2,0:T(8,128)(2,1)} %copy.46) | copy-start | bytes 3538948
  347.0 3.0 collective-permute-start
Sparse Core Ops, SparseCore 0:
  8.9 38.7 all-gather.11
  101.4 36.0 all-gather.7
  198.1 34.1 all-gather.13
  274.2 36.0 all-gather.9
where the time goes:
time: 364 us; the launch traced here: 359 us
  waiting for transfers between devices  137 us (38%)
  blocking collectives  73.5 us (20%)
  matrix products  70.3 us (19%)
  local copies, waits for them, and re-layouts  41.4 us (11%)
  other arithmetic  19.1 us (5%)
  between operations  15.5 us (4%)
    all_gather x1, waiting for transfers between devices, shards(): lax.all_gather(attended_time, 'heads', axis=1, tiled=True)  36.2 us
    all_gather x1, waiting for transfers between devices, shards(): lax.all_gather(attended, 'heads', axis=1, tiled=True)  36 us
    all_gather x1, waiting for transfers between devices, shards(): lax.all_gather(own_rows, 'heads', axis=1, tiled=True)  34.1 us
    all_to_all x1, blocking collectives, shards(): lax.all_to_all(after_spatial, 'seq', split_axis=2, concat_axis=0, tiled=T...  33 us
    all_to_all x1, blocking collectives, shards(): lax.all_to_all(block_out, 'seq', split_axis=0, concat_axis=2, tiled=True)  32.8 us
    all_gather x1, waiting for transfers between devices, shards(): video_piece = lax.all_gather(frame_tokens, 'heads', axis=1, tiled=True)  28.1 us
    dot_general x2, matrix products, block_step(): jnp.einsum('hpk,hek->hep', weights, value_rows[frame_id], preferred_eleme...  19.7 us
    unnamed x19, local copies, waits for them, and re-layouts  17.8 us
  transfers between devices with their start and end apart: 5, of which 5 were waited for; matrix products, arithmetic and copies ran while one was open for 1% of the time, Pallas kernels for 0%

commit v1 on v0

--- a/solution.py
+++ b/solution.py
@@ -114,7 +114,14 @@
     )
     attended_time = attended_time.astype(jnp.bfloat16).reshape(frames_all, width, columns)
     update_time = add_mixed(
-        lax.all_gather(attended_time, "heads", axis=1, tiled=True), temporal_out
+        jnp.roll(
+            jnp.concatenate(
+                [attended_time, lax.ppermute(attended_time, "heads", [(0, 1), (1, 0)])], axis=1
+            ),
+            lax.axis_index("heads") * attended_time.shape[1],
+            axis=1,
+        ),
+        temporal_out,
     )
     block_out = (own_rows.astype(jnp.float32) + update_time).astype(jnp.bfloat16)
     returned = lax.all_to_all(block_out, "seq", split_axis=0, concat_axis=2, tiled=True)

time: 364 us -> 357 us (0.981)
  waiting for transfers between devices: 137 us -> 128 us
    all_gather x1 -> x0, waiting for transfers between devices: 36.2 us -> none  [shards(): lax.all_gather(attended_time, 'heads', axis=1, tiled=True)]
    ppermute x0 -> x1, waiting for transfers between devices: none -> 27.5 us  [shards(): lax.ppermute(attended_time, 'heads', [(0, 1), (1, 0)])]
where the time goes in v1:
time: 357 us; the launch traced here: 352 us
  waiting for transfers between devices  128 us (36%)
  blocking collectives  72.8 us (20%)
  matrix products  72.3 us (20%)
  local copies, waits for them, and re-layouts  41.6 us (12%)
  other arithmetic  19.1 us (5%)
  between operations  15.6 us (4%)
    all_gather x1, waiting for transfers between devices, shards(): lax.all_gather(attended, 'heads', axis=1, tiled=True)  36 us
    all_gather x1, waiting for transfers between devices, shards(): lax.all_gather(own_rows, 'heads', axis=1, tiled=True)  34.3 us
    all_to_all x1, blocking collectives, shards(): lax.all_to_all(after_spatial, 'seq', split_axis=2, concat_axis=0, tiled=T...  33.2 us
    all_to_all x1, blocking collectives, shards(): lax.all_to_all(block_out, 'seq', split_axis=0, concat_axis=2, tiled=True)  31.9 us
    all_gather x1, waiting for transfers between devices, shards(): video_piece = lax.all_gather(frame_tokens, 'heads', axis=1, tiled=True)  28.1 us
    ppermute x1, waiting for transfers between devices, shards(): lax.ppermute(attended_time, 'heads', [(0, 1), (1, 0)])  27.5 us
    dot_general x2, matrix products, block_step(): jnp.einsum('hpk,hek->hep', weights, value_rows[frame_id], preferred_eleme...  19.7 us
    unnamed x19, local copies, waits for them, and re-layouts  17.8 us
  transfers between devices with their start and end apart: 5, of which 5 were waited for; matrix products, arithmetic and copies ran while one was open for 1% of the time, Pallas kernels for 0%

profile of v1, /device:TPU:0, one launch (start us, length us, event | category | flops | bytes accessed | tf_op | source)
XLA Modules:
  0.0 352.3 jit_solution(991237083070920224)
XLA Ops:
  6.5 0.0 copy-start
  6.5 0.0 all-gather.9.cloned.1.call-start
  6.5 0.7 all-gather.9.cloned.1.call-update
  7.3 0.0 all-gather.7.cloned.1.call-start
  7.3 0.7 convert_element_type.98
  8.7 7.7 %all-gather.1 = bf16[1,1,1152,128]{3,2,1,0:T(8,128)(2,1)S(1)} all-gather(bf16[1,1,576,128]{3,2,1,0:T(8,128)(2,1)} %param.14), channel_id=3, replica_groups=mesh['groups'=2,'seq'=4,'heads'=2,'cfg'=2] {'heads'}, dimensions={2}, use_global_device_ids=true | all-gather | bytes 442368 | tf_op jit(solution)/shard_map/all_gather | solution.py:55
  16.4 0.2 fusion.100
  16.6 3.0 fusion.94
  19.6 28.1 %all-gather.9.cloned.1.call-done = bf16[1,1,1152,1024]{3,2,1,0:T(8,128)(2,1)} async-done(((bf16[1,1,576,1024]{3,2,1,0:T(8,128)(2,1)}), bf16[1,1,1152,1024]{3,2,1,0:T(8,128)(2,1)}) %all-gather.9.cloned.1.call-update) | async-done | bytes 2359312 | tf_op jit(solution)/shard_map/all_gather | solution.py:54
  47.7 0.0 copy-start.3
  47.7 2.3 fusion.50
  50.0 0.0 copy-done.3
  50.1 7.3 %fusion.48 = bf16[1,1024,3,576]{1,3,2,0:T(8,128)(2,1)S(1)} fusion(f32[1024]{0:T(1024)S(1)} %add_rsqrt_fusion.1, bf16[3,576,1152]{2,1,0:T(8,128)(2,1)} %param.19, bf16[1,1,1152,1024]{3,2,1,0:T(8,128)(2,1)S(1)} %copy-done.3, f32[1152]{0:T(1024)S(1)} %convert_element_type.98), kind=kOutput, calls=%fused_computation.28 | convolution fusion | flops 4083941376 | bytes 9888256 | tf_op jit(solution)/shard_map/kod,fdp->fkop/dot_general | solution.py:26
  57.3 1.4 slice_bitcast_fusion
  58.7 1.3 pad_maximum_fusion
  60.1 37.1 %while.10 = (s32[]{:T(128)}, bf16[2,8,72,512]{3,2,1,0:T(8,128)(2,1)}, pred[1,1152]{1,0:T(4,128)(4,1)S(1)}, s32[2]{0:T(128)S(1)}, bf16[1,8,72,1024]{3,2,1,0:T(8,1...) while((s32[]{:T(128)}, ...), condition=%wide.region_5.6_spmd, body=%wide.region_2.5_spmd.sunk | while | flops 2081200384 | bytes 5788856 | solution.py:90
  60.6 0.7 dynamic_slice.87
  62.0 7.0 %exponential_reduce_fusion.2 = f32[8,512]{1,0:T(8,128)S(1)} fusion(pred[1152]{0:T(1024)(128)(4,1)S(1)} %reduce.5, bf16[1,8,72,1152]{3,2,1,0:T(8,128)(2,1)S(1)} %get-tuple-element.139, bf16[1,8,72,1024]{3,2,1,0:T(8,128)(2,1)} %get-tuple-element.138, s32[]{:T(128)S(6)} %select_n.67), kind=kOutput, calls=%fused_computation.5.clone.1 | convolution fusion | flops 698352768 | bytes 1934468 | tf_op jit(solution)/shard_map/while/body/eval_jaxpr/sub | solution.py:17
  69.0 9.8 %fusion.128 = bf16[2,8,72,512]{3,2,1,0:T(8,128)(2,1)} fusion(bf16[2,8,72,512]{3,2,1,0:T(8,128)(2,1)} %get-tuple-element.123, s32[]{:T(128)} %get-tuple-element.122, bf16[1,8,72,1152]{3,2,1,0:T(8,128)(2,1)} %get-tuple-element.140, f32[8,512]{1,0:T(8,128)S(1)} %exponential_reduce_fusion.2, pred[1152]{0:T(1024)(128)(4,1)S(1)} %reduce.5, ...), kind=kOutput, calls=%fused_computation.13.clone.1 | convolution fusion | flops 1382847616 | bytes 3851908 | tf_op jit(solution)/shard_map/while/body/eval_jaxpr/hpk,hek->hep/dot_general | solution.py:85
  78.9 0.7 dynamic_slice.87
  80.3 7.0 %exponential_reduce_fusion.2 = f32[8,512]{1,0:T(8,128)S(1)} fusion(pred[1152]{0:T(1024)(128)(4,1)S(1)} %reduce.5, bf16[1,8,72,1152]{3,2,1,0:T(8,128)(2,1)S(1)} %get-tuple-element.139, bf16[1,8,72,1024]{3,2,1,0:T(8,128)(2,1)} %get-tuple-element.138, s32[]{:T(128)S(6)} %select_n.67), kind=kOutput, calls=%fused_computation.5.clone.1 | convolution fusion | flops 698352768 | bytes 1934468 | tf_op jit(solution)/shard_map/while/body/eval_jaxpr/sub | solution.py:17
  87.3 9.8 %fusion.128 = bf16[2,8,72,512]{3,2,1,0:T(8,128)(2,1)} fusion(bf16[2,8,72,512]{3,2,1,0:T(8,128)(2,1)} %get-tuple-element.123, s32[]{:T(128)} %get-tuple-element.122, bf16[1,8,72,1152]{3,2,1,0:T(8,128)(2,1)} %get-tuple-element.140, f32[8,512]{1,0:T(8,128)S(1)} %exponential_reduce_fusion.2, pred[1152]{0:T(1024)(128)(4,1)S(1)} %reduce.5, ...), kind=kOutput, calls=%fused_computation.13.clone.1 | convolution fusion | flops 1382847616 | bytes 3851908 | tf_op jit(solution)/shard_map/while/body/eval_jaxpr/hpk,hek->hep/dot_general | solution.py:85
  97.2 2.5 copy.43
  99.6 1.7 reshape.105
  101.3 0.0 all-gather.7.cloned.1.call-update
  101.3 0.2 all-gather.11.cloned.1.call-start
  101.6 36.0 %all-gather.7.cloned.1.call-done = bf16[1,1152,1024]{2,1,0:T(8,128)(2,1)} async-done(((bf16[1,576,1024]{2,1,0:T(8,128)(2,1)}), bf16[1,1152,1024]{2,1,0:T(8,128)(2,1)}) %all-gather.7.cloned.1.call-update) | async-done | bytes 2359312 | tf_op jit(solution)/shard_map/all_gather | solution.py:93
  137.5 0.0 copy-done
  137.5 3.7 %fusion.69 = bf16[1,576,1024]{2,1,0:T(8,128)(2,1)S(1)} fusion(bf16[576,1152]{1,0:T(8,128)(2,1)S(1)} %copy-done, bf16[1,1152,1024]{2,1,0:T(8,128)(2,1)} %all-gather.7.cloned.1.call-done, bf16[1,1,576,1024]{3,2,1,0:T(8,128)(2,1)} %param.13), kind=kOutput, calls=%fused_computation.55 | convolution fusion | flops 1360723968 | bytes 6045696 | tf_op jit(solution)/shard_map/oc,fcp->fop/dot_general | solution.py:31
  141.2 4.1 %copy.44 = bf16[1,576,1024]{1,0,2:T(2,128)(2,1)} copy(bf16[1,576,1024]{2,1,0:T(8,128)(2,1)S(1)} %fusion.69) | data formatting | bytes 2359296 | tf_op jit(solution)/shard_map/convert_element_type | solution.py:94
  145.3 0.5 broadcast.82
  145.8 9.9 %reduce.3 = bf16[1024,576]{1,0:T(8,128)(2,1)S(1)} reduce(bf16[1024,1,576]{2,1,0:T(2,128)(2,1)} %bitcast.188, bf16[]{:T(256)} %broadcast.82), dimensions={1}, to_apply=%bitcast.164.reduce_sub_computation | reduce | bytes 2359298
  155.8 2.6 reshape.124
  158.4 33.2 %all_to_all.36 = bf16[4,2,73728]{2,1,0:T(2,128)(2,1)S(1)} all-to-all(bf16[4,2,73728]{2,1,0:T(2,128)(2,1)} %reshape.124), channel_id=1, replica_groups=mesh['groups'=2,'seq'=4,'heads'=2,'cfg'=2] {'seq'}, dimensions={0} | all-to-all | bytes 2359296 | tf_op jit(solution)/shard_map/all_to_all | solution.py:95
  191.6 3.3 reshape.125
  194.8 1.9 copy.57
  196.8 0.0 copy-start.5
  196.8 1.5 copy.46
  198.2 0.0 all-gather.11.cloned.1.call-update
  198.2 0.0 copy-done.5
  198.3 34.3 %all-gather.11.cloned.1.call-done = bf16[4,1,1152,256]{3,2,0,1:T(8,128)(2,1)} async-done(((bf16[4,1,576,256]{3,2,0,1:T(8,128)(2,1)}), bf16[4,1,1152,256]{3,2,0,1:T(8,128)(2,1)}) %all-gather.11.cloned.1.call-update) | async-done | bytes 2359312 | tf_op jit(solution)/shard_map/all_gather | solution.py:99
  232.6 2.3 fusion.52
  234.9 0.1 copy-done.4
  234.9 7.2 %multiply_convert_fusion = bf16[4,256,3,576]{1,3,2,0:T(8,128)(2,1)S(1)} fusion(f32[4,256]{1,0:T(4,128)S(1)} %add_rsqrt_fusion, bf16[3,576,1152]{2,1,0:T(8,128)(2,1)} %param.22, bf16[4,1,1152,256]{3,2,0,1:T(8,128)(2,1)S(1)} %copy-done.4, f32[1152]{0:T(1024)S(1)} %convert_element_type.109), kind=kOutput, calls=%fused_computation.29 | convolution fusion | flops 4083941376 | bytes 9888256 | tf_op jit(solution)/shard_map/kod,fdp->fkop/dot_general | solution.py:26
  242.2 1.9 fusion.113
  244.1 2.8 copy.59
  246.9 4.1 %copy.60 = bf16[4,1,8,72,256]{3,0,4,2,1:T(4,128)(2,1)} copy(bf16[4,1,8,72,256]{4,3,2,1,0:T(8,128)(2,1)} %get-tuple-element.59) | data formatting | bytes 2359296
  251.0 5.8 %fusion.76 = f32[8,256,4,4]{3,2,1,0:T(4,128)} fusion(bf16[4,1,8,72,256]{3,0,4,2,1:T(4,128)(2,1)} %copy.60, bf16[4,1,8,72,256]{3,0,4,2,1:T(4,128)(2,1)S(1)} %copy.59), kind=kOutput, calls=%fused_computation.62 | convolution fusion | flops 4718592 | bytes 2490368 | tf_op jit(solution)/shard_map/fhep,ghep->hfgp/dot_general | solution.py:108
  256.8 2.8 copy.50
  259.7 0.0 copy-start.1
  259.8 2.1 copy.51
  261.9 0.0 copy-done.1
  261.9 2.5 copy.58
  264.3 5.8 %convert_bitcast_fusion = bf16[4,8,72,256]{2,0,3,1:T(4,128)(2,1)} fusion(bf16[8,4,4,256]{2,1,3,0:T(4,128)(2,1)} %copy.51, bf16[4,1,8,72,256]{3,0,4,2,1:T(4,128)(2,1)} %copy.58), kind=kOutput, calls=%fused_computation.67 | convolution fusion | flops 5308416 | bytes 2424832 | tf_op jit(solution)/shard_map/hfgp,ghep->fhep/dot_general | solution.py:112
  270.2 4.4 %copy.52 = bf16[4,8,72,256]{3,2,1,0:T(8,128)(2,1)} copy(bf16[4,8,72,256]{2,0,3,1:T(4,128)(2,1)} %convert_bitcast_fusion) | data formatting | bytes 2359296 | tf_op jit(solution)/shard_map/convert_element_type | solution.py:115
  274.6 0.4 collective-permute-start
  275.0 27.5 %collective-permute-done = bf16[4,576,256]{2,1,0:T(8,128)(2,1)} collective-permute-done((bf16[4,576,256]{2,1,0:T(8,128)(2,1)}, bf16[4,576,256]{2,1,0:T(8,128)(2,1)}, u32[]{:S(2)}, u32[]{:S(2)}) %collective-permute-start) | collective-permute-done | bytes 1179680 | tf_op jit(solution)/shard_map/ppermute | solution.py:119
  302.5 0.0 copy-done.2
  302.5 5.7 %fusion.68 = bf16[4,576,256]{2,1,0:T(8,128)(2,1)S(1)} fusion(s32[]{:T(128)S(6)} %select_n.42, bf16[4,576,256]{2,1,0:T(8,128)(2,1)} %bitcast.198, bf16[4,576,256]{2,1,0:T(8,128)(2,1)} %collective-permute-done, bf16[576,1152]{1,0:T(8,128)(2,1)} %param.23, bf16[1,576,4,256]{3,1,2,0:T(8,128)(2,1)S(1)} %copy-done.2), kind=kOutput, calls=%fused_computation.53 | convolution fusion | flops 1370161152 | bytes 6045700 | tf_op jit(solution)/shard_map/oc,fcp->fop/dot_general | solution.py:31
  308.2 31.9 %all_to_all.37 = bf16[4,576,256]{2,1,0:T(8,128)(2,1)S(1)} all-to-all(bf16[4,576,256]{2,1,0:T(8,128)(2,1)S(1)} %fusion.68), channel_id=1, replica_groups=mesh['groups'=2,'seq'=4,'heads'=2,'cfg'=2] {'seq'}, dimensions={0} | all-to-all | bytes 2359296 | tf_op jit(solution)/shard_map/all_to_all | solution.py:127
  340.2 0.1 copy.61
  340.3 0.1 collective-permute-start.1
  341.7 1.6 collective-permute-done.1
  343.4 2.2 fusion.98
  (16 shorter events, 0.2 us)
Async XLA Ops:
  6.5 131.0 %copy-start = (bf16[576,1152]{1,0:T(8,128)(2,1)S(1)}, bf16[576,1152]{1,0:T(8,128)(2,1)}, u32[]{:S(2)}) copy-start(bf16[576,1152]{1,0:T(8,128)(2,1)} %param.20) | copy-start | bytes 3981316
  6.5 41.1 %all-gather.9.cloned.1.call-start = ((), (), s32[]{:S(2)}) async-start(), calls=%async_computation.3 | async-start | bytes 3538944 | tf_op jit(solution)/shard_map/all_gather | solution.py:54
  7.3 130.3 %all-gather.7.cloned.1.call-start = ((), (), s32[]{:S(2)}) async-start(), calls=%async_computation.2 | async-start | bytes 3538944 | tf_op jit(solution)/shard_map/all_gather | solution.py:93
  47.7 2.4 copy-start.3
  101.3 131.2 %all-gather.11.cloned.1.call-start = ((), (), s32[]{:S(2)}) async-start(), calls=%async_computation.4 | async-start | bytes 3538944 | tf_op jit(solution)/shard_map/all_gather | solution.py:99
  196.8 1.5 copy-start.5
  232.6 2.4 copy-start.4
  259.7 2.2 copy-start.1
  270.2 32.3 %copy-start.2 = (bf16[1,576,4,256]{3,1,2,0:T(8,128)(2,1)S(1)}, bf16[1,576,4,256]{3,1,2,0:T(8,128)(2,1)}, u32[]{:S(2)}) copy-start(bf16[1,576,4,256]{3,1,2,0:T(8,128)(2,1)} %copy.46) | copy-start | bytes 3538948
  274.6 27.9 %collective-permute-start = (bf16[4,576,256]{2,1,0:T(8,128)(2,1)}, bf16[4,576,256]{2,1,0:T(8,128)(2,1)}, u32[]{:S(2)}, u32[]{:S(2)}) collective-permute-start(bf16[4,576,256]{2,1,0:T(8,128)(2,1)} %bitcast.197), channel_id=1, source_target_pairs={{0,2},{2,0},{1,3},{3,1},{4,6},{6,4},{5,7},{7,5},{8,10},{10,8},{9,1... | collective-permute-start | bytes 3538952 | tf_op jit(solution)/shard_map/ppermute | solution.py:119
  340.3 3.0 collective-permute-start.1
Sparse Core Ops, SparseCore 0:
  8.9 38.7 all-gather.8
  101.4 36.0 all-gather.6
  198.4 34.1 all-gather.10
